TPU v7x, 128 devices: a whole 4x4x4 slice. The times are simulated.
128 devices in a mesh: row: 8 (over z, core), col: 16 (over y, x).
Axes of the slice: x: 4, y: 4, z: 4, core: 2. Of those that a mesh axis runs over, the one named last changes fastest.
Arguments:
- item_table: float32 [5242880, 128], P(('row', 'col')), may hold values from -6 to 6
- owner_ids: int32 [16384, 50], P(('row', 'col')), may hold values from 0 to 127, as said below
- row_ids: int32 [16384, 50], P(('row', 'col')), may hold values from 0 to 40959
- lengths: int32 [16384], P(('row', 'col')), may hold values from 25 to 50
- dense_input: bfloat16 [16384, 256], P(('row', 'col')), may hold values from -6 to 6
- w_bottom: bfloat16 [256, 256], replicated, may hold values from -0.375 to 0.375
Outputs:
- features: float32 [16384, 384], P(('row', 'col'))
Inputs may be any that keep to these rules, and one draw needn't show every extreme that they name: Among the live positions (p < lengths[u]) of the 128 users of one device, at most 75 have the same owner_ids value; in every draw some owner_ids values receive exactly 75 live positions from every device.
All inputs are finite; a program needn't handle non-finite values.
Results may differ from a plain program's by a relative error of at most 0.0003.
Values sent between devices are 32-bit elements; how exact they have to be, the bound alone decides.
No kernel may reach another device: no remote copies, remote signals or barrier semaphores. Data moves between devices by JAX's collectives and lax.ppermute only.
A program may use at most 128 MiB of HBM per device.

v0:
```python
import jax
import jax.numpy as jnp
from jax import lax
from jax.sharding import PartitionSpec as P

HIGH = lax.Precision.HIGHEST


def to_owners(buffer):
    return lax.all_to_all(buffer, ("row", "col"), split_axis=0, concat_axis=0, tiled=True)


def to_homes(fetched):
    return lax.all_to_all(fetched, ("row", "col"), split_axis=0, concat_axis=0, tiled=True)


def strict_lower(count):
    later = lax.broadcasted_iota(jnp.int32, (count, count), 0)
    earlier = lax.broadcasted_iota(jnp.int32, (count, count), 1)
    return (later > earlier).astype(jnp.float32)


def per_device(item_table, owner_ids, row_ids, lengths, dense_input, w_bottom):
    user_count, hist_len = owner_ids.shape
    pos_count = user_count * hist_len
    owner_count = lax.axis_size("row") * lax.axis_size("col")
    capacity = 3 * pos_count // (2 * owner_count)
    slot_total = owner_count * capacity
    position = lax.broadcasted_iota(jnp.int32, (user_count, hist_len), 1)
    live_mask = position < lengths[:, None]
    owner_iota = lax.broadcasted_iota(jnp.int32, (1, 1, owner_count), 2)
    assign = ((owner_ids[:, :, None] == owner_iota) & live_mask[:, :, None]).astype(jnp.float32)
    within = jnp.einsum("hk,uko->uho", strict_lower(hist_len), assign, precision=HIGH)
    per_user = jnp.sum(assign, axis=1)
    offsets = jnp.dot(strict_lower(user_count), per_user, precision=HIGH)
    rank = jnp.sum(assign * (within + offsets[:, None, :]), axis=2)
    rank_iota = lax.broadcasted_iota(jnp.int32, (1, 1, capacity), 2).astype(jnp.float32)
    spot = ((rank[:, :, None] == rank_iota) & live_mask[:, :, None]).astype(jnp.float32)
    hidden = jnp.dot(dense_input, w_bottom, preferred_element_type=jnp.float32)
    dense_out = jax.nn.silu(hidden)
    weighted = spot * row_ids.astype(jnp.float32)[:, :, None]
    buffer = jnp.einsum("uho,uhc->oc", assign, weighted, precision=HIGH).astype(jnp.int32)
    arrived = to_owners(buffer)
    fetched = jnp.take(item_table, arrived.reshape(-1), axis=0).reshape(owner_count, capacity, -1)
    returned = to_homes(fetched).reshape(slot_total, -1)
    selector = jnp.einsum("uho,uhc->uoc", assign, spot, precision=HIGH).reshape(
        user_count, slot_total
    )
    totals = jnp.dot(selector, returned, precision=HIGH)
    pooled = totals / lengths[:, None].astype(jnp.float32)
    return jnp.concatenate([pooled, dense_out], axis=1)


def solution(mesh):
    in_specs = (
        P(("row", "col"), None),
        P(("row", "col"), None),
        P(("row", "col"), None),
        P(("row", "col")),
        P(("row", "col"), None),
        P(),
    )
    out_specs = P(("row", "col"), None)
    return jax.shard_map(
        per_device, mesh=mesh, in_specs=in_specs, out_specs=out_specs, check_vma=False
    )
```

profile of v0, /device:TPU:1, one launch (start us, length us, event | category | flops | bytes accessed | tf_op | source)
XLA Modules:
  0.0 158.9 jit_solution(17920177087260549754)
XLA Ops:
  0.0 0.0 copy-start
  0.0 0.8 iota_compare_fusion.2
  0.8 0.8 copy.17
  1.6 2.5 %convert_reduce_fusion = f32[128,128]{1,0:T(8,128)S(1)} fusion(pred[128,50]{1,0:T(8,128)(4,1)S(1)} %iota_compare_fusion.2, s32[128,50]{1,0:T(8,128)S(1)} %copy.17), kind=kLoop, calls=%fused_computation.3 | loop fusion | flops 3260416 | bytes 97536 | tf_op jit(solution)/shard_map/reduce_sum | solution.py:34
  4.2 2.5 %fusion.1 = pred[128,50,128]{2,1,0:T(8,128)(4,1)S(1)} fusion(s32[128,50]{1,0:T(8,128)S(1)} %copy.17, pred[128,50]{1,0:T(8,128)(4,1)S(1)} %iota_compare_fusion.2), kind=kLoop, calls=%fused_computation.5 | loop fusion | flops 1638400 | bytes 851200 | tf_op jit(solution)/shard_map/and | solution.py:32
  6.7 0.1 copy.19
  6.8 0.2 fusion.23
  7.0 0.0 copy-start.1
  7.0 7.5 %fusion = f32[128,50]{1,0:T(8,128)S(1)} fusion(f32[128,128]{1,0:T(8,128)S(1)} %fusion.23, pred[128,50]{1,0:T(8,128)(4,1)S(1)} %iota_compare_fusion.2, s32[128,50]{1,0:T(8,128)S(1)} %copy.17), kind=kOutput, calls=%fused_computation.2 | convolution fusion | flops 87650496 | bytes 123136 | tf_op jit(solution)/shard_map/hk,uko->uho/dot_general | solution.py:33
  14.5 0.1 copy.18
  14.6 0.0 copy-done.1
  14.6 1.7 %fusion.16 = s32[128,1,75]{0,2,1:T(8,128)S(1)} fusion(pred[128,50,128]{2,1,0:T(8,128)(4,1)S(1)} %fusion.1, f32[128,50]{0,1:T(8,128)S(1)} %convert_element_type.26, f32[128,50]{0,1:T(8,128)S(1)} %copy.18, f32[75]{0:T(128)S(1)} %iota_convert_fusion, pred[128,50]{0,1:T(8,128)(4,1)S(1)} %copy.19), kind=kOutput, calls=%fused_computation.15 | convolution fusion | flops 738729600 | bytes 915500 | tf_op jit(solution)/shard_map/uho,uhc->oc/dot_general | solution.py:42
  16.4 0.1 copy.22
  16.5 20.9 %all_to_all.14 = s32[128,1,75]{2,1,0:T(1,128)S(1)} all-to-all(s32[128,1,75]{2,1,0:T(1,128)S(1)} %copy.22), channel_id=1, replica_groups=mesh['row'=8,'col'=16] {'row','col'}, dimensions={0} | all-to-all | bytes 76800 | tf_op jit(solution)/shard_map/all_to_all | solution.py:10
  37.4 0.5 broadcast.72
  37.9 0.8 reduce.5
  38.7 0.2 reshape.83
  38.9 0.1 fusion.24
  39.1 25.5 %gather_fusion = f32[9600,128]{1,0:T(8,128)} fusion(f32[40960,128]{1,0:T(8,128)} %param.6, s32[10240]{0:T(1024)S(1)} %pad_clamp_fusion), kind=kCustom, calls=%fused_computation | custom fusion | bytes 9868800 | tf_op jit(solution)/shard_map/jit(_take)/gather | solution.py:44
  64.5 5.2 %gather.7 = f32[128,75,128]{2,1,0:T(8,128)} reshape(f32[9600,128]{1,0:T(8,128)} %gather_fusion) | data formatting | bytes 9830400 | tf_op jit(solution)/shard_map/jit(_take)/gather | solution.py:44
  69.8 7.4 %broadcast_select_fusion = f32[128,75,128]{2,1,0:T(8,128)} fusion(f32[128,75,128]{2,1,0:T(8,128)} %gather.7, pred[128,75]{1,0:T(8,128)(4,1)S(1)} %compare_and_fusion.1), kind=kLoop, calls=%fused_computation.8 | loop fusion | flops 1228800 | bytes 9840000 | tf_op jit(solution)/shard_map/jit(_take)/select_n | solution.py:44
  77.2 0.0 copy-start.2
  77.2 5.6 %all-to-all-start.1 = ((f32[128,75,128]{2,1,0:T(8,128)}), f32[128,75,128]{2,1,0:T(8,128)}, u32[]{:S(2)}, u32[]{:S(2)}) async-start(f32[128,75,128]{2,1,0:T(8,128)} %broadcast_select_fusion), calls=%async_computation.1 | async-start | bytes 10485760 | tf_op jit(solution)/shard_map/all_to_all | solution.py:14
  82.8 0.0 copy-done.2
  82.9 0.4 compare_and_fusion
  83.3 3.0 %copy.20 = pred[128,50,75]{2,1,0:T(8,128)(4,1)S(1)} copy(pred[128,50,75]{0,2,1:T(8,128)(4,1)S(1)} %compare_and_fusion) | data formatting | bytes 960000 | tf_op jit(solution)/shard_map/and | solution.py:38
  86.3 6.6 %fusion.28 = f32[128,128,75]{1,2,0:T(8,128)} fusion(pred[128,50,75]{2,1,0:T(8,128)(4,1)S(1)} %copy.20, s32[128,50]{1,0:T(8,128)S(1)} %copy.17, pred[128,50]{1,0:T(8,128)(4,1)S(1)} %iota_compare_fusion.2), kind=kOutput, calls=%fused_computation.32 | convolution fusion | flops 124518400 | bytes 5427200 | tf_op jit(solution)/shard_map/uho,uhc->uoc/dot_general | solution.py:46
  92.9 0.0 copy-start.3
  92.9 6.5 %copy.26 = f32[128,128,75]{0,2,1:T(8,128)} copy(f32[128,128,75]{1,2,0:T(8,128)} %fusion.28) | data formatting | bytes 9830400 | tf_op jit(solution)/shard_map/uho,uhc->uoc/dot_general | solution.py:46
  99.3 0.0 copy-done
  99.3 0.0 copy-done.3
  99.3 0.2 divide_multiply_fusion
  99.5 46.2 %all-to-all-done.1 = f32[128,75,128]{2,1,0:T(8,128)} async-done(((f32[128,75,128]{2,1,0:T(8,128)}), f32[128,75,128]{2,1,0:T(8,128)}, u32[]{:S(2)}, u32[]{:S(2)}) %all-to-all-start.1) | async-done | bytes 4915232 | tf_op jit(solution)/shard_map/all_to_all | solution.py:14
  145.8 12.4 %fusion.5 = f32[128,128]{0,1:T(8,128)S(1)} fusion(f32[128,128,75]{0,2,1:T(8,128)} %copy.26, f32[128,75,128]{2,1,0:T(8,128)} %all-to-all-done.1, f32[128]{0:T(128)S(1)} %convert_element_type.28), kind=kOutput, calls=%fused_computation.12 | convolution fusion | flops 1887453184 | bytes 9896448 | tf_op jit(solution)/shard_map/dot_general | solution.py:49
  158.1 0.1 copy.25
  158.2 0.7 pad_maximum_fusion
  (5 shorter events, 0.0 us)
Async XLA Ops:
  0.0 99.3 %copy-start = (bf16[256,256]{1,0:T(8,128)(2,1)S(1)}, bf16[256,256]{1,0:T(8,128)(2,1)}, u32[]{:S(2)}) copy-start(bf16[256,256]{1,0:T(8,128)(2,1)} %param.11) | copy-start | bytes 393220
  7.0 7.6 %copy-start.1 = (s32[128,50]{0,1:T(8,128)S(1)}, s32[128,50]{0,1:T(8,128)}, u32[]{:S(2)}) copy-start(s32[128,50]{0,1:T(8,128)} %param.8) | copy-start | bytes 76804
  77.2 5.6 %copy-start.2 = (s32[128]{0:T(128)S(1)}, s32[128]{0:T(128)}, u32[]{:S(2)}) copy-start(s32[128]{0:T(128)} %param.9) | copy-start | bytes 1540
  77.2 68.6 %all-to-all-start.1 = ((f32[128,75,128]{2,1,0:T(8,128)}), f32[128,75,128]{2,1,0:T(8,128)}, u32[]{:S(2)}, u32[]{:S(2)}) async-start(f32[128,75,128]{2,1,0:T(8,128)} %broadcast_select_fusion), calls=%async_computation.1 | async-start | bytes 10485760 | tf_op jit(solution)/shard_map/all_to_all | solution.py:14
  92.9 6.5 %copy-start.3 = (bf16[128,256]{1,0:T(8,128)(2,1)S(1)}, bf16[128,256]{1,0:T(8,128)(2,1)}, u32[]{:S(2)}) copy-start(bf16[128,256]{1,0:T(8,128)(2,1)} %param.10) | copy-start | bytes 196612
where the time goes:
time: 160 us; the launch traced here: 159 us
  waiting for transfers between devices  46.2 us (29%)
  local copies, waits for them, and re-layouts  42.1 us (26%)
  matrix products  28.6 us (18%)
  blocking collectives  20.9 us (13%)
  other arithmetic  15.4 us (10%)
  starting transfers between devices  5.63 us (4%)
    all_to_all x1, waiting for transfers between devices, to_homes(): lax.all_to_all(fetched, ('row', 'col'), split_axis=0, concat_axis=0, tile...  46.2 us
    gather x2, local copies, waits for them, and re-layouts, per_device(): jnp.take(item_table, arrived.reshape(-1), axis=0)  30.7 us
    all_to_all x1, blocking collectives, to_owners(): lax.all_to_all(buffer, ('row', 'col'), split_axis=0, concat_axis=0, tiled...  20.9 us
    dot_general x1, matrix products, per_device(): totals = jnp.dot(selector, returned, precision=HIGH)  12.4 us
    select_n x2, other arithmetic, per_device(): jnp.take(item_table, arrived.reshape(-1), axis=0)  7.56 us
    dot_general x1, matrix products, per_device(): jnp.einsum('hk,uko->uho', strict_lower(hist_len), assign, precision=HIGH)  7.54 us
    dot_general x1, matrix products, per_device(): jnp.einsum('uho,uhc->uoc', assign, spot, precision=HIGH)  6.61 us
    dot_general x1, local copies, waits for them, and re-layouts, per_device(): jnp.einsum('uho,uhc->uoc', assign, spot, precision=HIGH)  6.45 us
  transfers between devices with their start and end apart: 1, of which 1 were waited for; matrix products, arithmetic and copies ran while one was open for 10% of the time, Pallas kernels for 0%

commit v1 on v0

v1 whole, which is shorter than its diff:
```python
import functools

import jax
import jax.numpy as jnp
from jax import lax
from jax.experimental import pallas as pl
from jax.experimental.pallas import tpu as pltpu
from jax.sharding import PartitionSpec as P

SLOT_PAD = 80
LANES = 128
FIRST_SLOTS = 20


def round_up(value, unit):
    return (value + unit - 1) // unit * unit


def exchange(buffer):
    return lax.all_to_all(buffer, ("row", "col"), split_axis=0, concat_axis=0, tiled=True)


def route_kernel(me_ref, owner_ref, row_ref, len_ref, rows_out, users_out, assign_ref, value_ref):
    hist_len, user_count = owner_ref.shape
    owner_count = rows_out.shape[0]
    lens = len_ref[...]
    owner_iota = lax.broadcasted_iota(jnp.int32, (owner_count, user_count), 0)
    slot_iota = lax.broadcasted_iota(jnp.int32, (SLOT_PAD, user_count), 0)
    user_iota = lax.broadcasted_iota(jnp.int32, (1, user_count), 1)
    earlier = lax.broadcasted_iota(jnp.int32, (user_count, 2 * user_count), 0)
    later = lax.broadcasted_iota(jnp.int32, (user_count, 2 * user_count), 1)
    counter = jnp.where((earlier < later) | (later >= user_count), 1.0, 0.0).astype(jnp.bfloat16)
    offset = jnp.zeros((owner_count, user_count), jnp.float32)
    for h in range(hist_len):
        owners = jnp.where(h < lens, owner_ref[h : h + 1, :], -1)
        hits = owners == owner_iota
        assign = jnp.where(hits, 1.0, 0.0).astype(jnp.bfloat16)
        assign_ref[:, h * user_count : (h + 1) * user_count] = assign
        counts = jnp.dot(assign, counter, preferred_element_type=jnp.float32)
        ahead = counts[:, :user_count] + offset
        rank = jnp.sum(jnp.where(hits, ahead, 0.0), axis=0, keepdims=True).astype(jnp.int32)
        offset = offset + counts[:, user_count:]
        spot = rank == slot_iota
        rows = row_ref[h : h + 1, :]
        high = (rows >> 8).astype(jnp.float32)
        low = (rows & 255).astype(jnp.float32)
        name = (user_iota + 1).astype(jnp.float32)
        for part, content in enumerate((high, low, name)):
            value_ref[part * SLOT_PAD : (part + 1) * SLOT_PAD, h * user_count : (h + 1) * user_count] = (
                jnp.where(spot, content, 0.0).astype(jnp.bfloat16)
            )
    packed = lax.dot_general(
        assign_ref[...], value_ref[...], (((1,), (1,)), ((), ())), preferred_element_type=jnp.float32
    )
    names = packed[:, 2 * SLOT_PAD :]
    spare = me_ref[0, 0] * SLOT_PAD + lax.broadcasted_iota(jnp.int32, names.shape, 1)
    table_rows = (packed[:, :SLOT_PAD] * 256.0 + packed[:, SLOT_PAD : 2 * SLOT_PAD]).astype(jnp.int32)
    table_rows = jnp.where(names > 0.0, table_rows, spare)
    fill = jnp.zeros((owner_count, LANES - SLOT_PAD), jnp.int32)
    rows_out[...] = jnp.concatenate([table_rows, fill], axis=1)
    users_out[...] = jnp.concatenate([names.astype(jnp.int32), fill], axis=1)


def route(me, owner_t, row_t, lengths, owner_count):
    hist_len, user_count = owner_t.shape
    pos_count = hist_len * user_count
    shape = jax.ShapeDtypeStruct((owner_count, LANES), jnp.int32)
    return pl.pallas_call(
        route_kernel,
        in_specs=[
            pl.BlockSpec(memory_space=pltpu.SMEM),
            pl.BlockSpec(memory_space=pltpu.VMEM),
            pl.BlockSpec(memory_space=pltpu.VMEM),
            pl.BlockSpec(memory_space=pltpu.VMEM),
        ],
        out_shape=(shape, shape),
        scratch_shapes=[
            pltpu.VMEM((owner_count, pos_count), jnp.bfloat16),
            pltpu.VMEM((3 * SLOT_PAD, pos_count), jnp.bfloat16),
        ],
        name="route",
    )(jnp.full((1, 1), me, jnp.int32), owner_t, row_t, lengths.reshape(1, user_count))


def fetch_kernel(first, count, groups, wanted_ref, table_ref, out_ref, stage_ref, in_sems, out_sems):
    sources = wanted_ref.shape[0]
    per_group = sources // groups
    span = per_group * count

    def issue(group):
        def one_source(index, carry):
            source = group * per_group + index
            for c in range(count):
                pltpu.make_async_copy(
                    table_ref.at[pl.ds(wanted_ref[source, 0, first + c], 1), :],
                    stage_ref.at[pl.ds(source * count + c, 1), :],
                    in_sems.at[group],
                ).start(priority=c % 2)
            return carry

        lax.fori_loop(0, per_group, one_source, 0)

    def store(group):
        place = pl.ds(group * span, span)
        return pltpu.make_async_copy(stage_ref.at[place, :], out_ref.at[place, :], out_sems.at[group])

    def arrive(group):
        place = pl.ds(group * span, span)
        pltpu.make_async_copy(table_ref.at[pl.ds(0, span), :], stage_ref.at[place, :], in_sems.at[group]).wait()
        store(group).start()

    for group in range(groups):
        issue(group)
        if group > 0:
            arrive(group - 1)
    arrive(groups - 1)
    for group in range(groups):
        store(group).wait()


def fetch(wanted, item_table, first, count, groups):
    sources = wanted.shape[0]
    dim = item_table.shape[1]
    return pl.pallas_call(
        functools.partial(fetch_kernel, first, count, groups),
        in_specs=[pl.BlockSpec(memory_space=pltpu.SMEM), pl.BlockSpec(memory_space=pl.ANY)],
        out_specs=pl.BlockSpec(memory_space=pl.ANY),
        out_shape=jax.ShapeDtypeStruct((sources * count, dim), jnp.float32),
        scratch_shapes=[
            pltpu.VMEM((sources * count, dim), jnp.float32),
            pltpu.SemaphoreType.DMA((groups,)),
            pltpu.SemaphoreType.DMA((groups,)),
        ],
        cost_estimate=pl.CostEstimate(
            flops=sources * count * 4000, bytes_accessed=sources * count * dim * 8, transcendentals=0
        ),
        name="fetch",
    )(wanted, item_table)


def add_rows(slot_ref, rows_ref, acc_ref):
    user_count = acc_ref.shape[0]
    rows = rows_ref[...]
    high = rows.astype(jnp.bfloat16)
    low = (rows - high.astype(jnp.float32)).astype(jnp.bfloat16)
    users = lax.broadcasted_iota(jnp.int32, (user_count, rows.shape[0]), 0) + 1
    selector = jnp.where(slot_ref[...] == users, 1.0, 0.0).astype(jnp.bfloat16)
    acc_ref[...] += jnp.dot(
        selector, jnp.concatenate([high, low], axis=1), preferred_element_type=jnp.float32
    )


def pool_first_kernel(slot_ref, rows_ref, acc_ref):
    @pl.when(pl.program_id(0) == 0)
    def _():
        acc_ref[...] = jnp.zeros_like(acc_ref)

    add_rows(slot_ref, rows_ref, acc_ref)


def pool_last_kernel(slot_ref, rows_ref, start_ref, len_ref, dense_ref, out_ref, acc_ref):
    step = pl.program_id(0)
    dim = rows_ref.shape[1]

    @pl.when(step == 0)
    def _():
        acc_ref[...] = start_ref[...]

    add_rows(slot_ref, rows_ref, acc_ref)

    @pl.when(step == pl.num_programs(0) - 1)
    def _():
        total = acc_ref[:, :dim] + acc_ref[:, dim:]
        out_ref[:, :dim] = total / len_ref[...]
        out_ref[:, dim:] = dense_ref[...]


def pool_first(slots, rows, user_count, steps):
    count, dim = rows.shape
    chunk = count // steps
    return pl.pallas_call(
        pool_first_kernel,
        grid=(steps,),
        in_specs=[pl.BlockSpec((1, chunk), lambda i: (0, i)), pl.BlockSpec((chunk, dim), lambda i: (i, 0))],
        out_specs=pl.BlockSpec((user_count, 2 * dim), lambda i: (0, 0)),
        out_shape=jax.ShapeDtypeStruct((user_count, 2 * dim), jnp.float32),
        cost_estimate=pl.CostEstimate(flops=count * 4000, bytes_accessed=count * dim * 4, transcendentals=0),
        name="pool_first",
    )(slots, rows)


def pool_last(slots, rows, start, lens, dense_out, steps):
    count, dim = rows.shape
    user_count, dense_dim = dense_out.shape
    chunk = count // steps
    return pl.pallas_call(
        pool_last_kernel,
        grid=(steps,),
        in_specs=[
            pl.BlockSpec((1, chunk), lambda i: (0, i)),
            pl.BlockSpec((chunk, dim), lambda i: (i, 0)),
            pl.BlockSpec((user_count, 2 * dim), lambda i: (0, 0)),
            pl.BlockSpec((user_count, dim), lambda i: (0, 0)),
            pl.BlockSpec((user_count, dense_dim), lambda i: (0, 0)),
        ],
        out_specs=pl.BlockSpec((user_count, dim + dense_dim), lambda i: (0, 0)),
        out_shape=jax.ShapeDtypeStruct((user_count, dim + dense_dim), jnp.float32),
        scratch_shapes=[pltpu.VMEM((user_count, 2 * dim), jnp.float32)],
        name="pool_last",
    )(slots, rows, start, lens, dense_out)


def per_device(item_table, owner_ids, row_ids, lengths, dense_input, w_bottom):
    user_count, hist_len = owner_ids.shape
    dim = item_table.shape[1]
    owner_count = lax.axis_size("row") * lax.axis_size("col")
    capacity = 3 * user_count * hist_len // (2 * owner_count)
    ahead = FIRST_SLOTS
    behind = capacity - ahead
    me = lax.axis_index("row") * lax.axis_size("col") + lax.axis_index("col")
    table_rows, slot_users = route(me, owner_ids.T, row_ids.T, lengths, owner_count)
    wanted = exchange(table_rows.reshape(owner_count, 1, LANES))
    fetched_one = fetch(wanted, item_table, 0, ahead, 4)
    fetched_two = fetch(wanted, item_table, ahead, behind, 8)
    returned_one = exchange(fetched_one.reshape(owner_count, ahead, 1, dim)).reshape(-1, dim)
    returned_two = exchange(fetched_two.reshape(owner_count, behind, 1, dim)).reshape(-1, dim)
    slots_one = slot_users[:, :ahead].reshape(1, owner_count * ahead)
    slots_two = slot_users[:, ahead:capacity].reshape(1, owner_count * behind)
    hidden = jnp.dot(dense_input, w_bottom, preferred_element_type=jnp.float32)
    dense_out = jax.nn.silu(hidden)
    lens = jnp.broadcast_to(lengths[:, None].astype(jnp.float32), (user_count, dim))
    start = pool_first(slots_one, returned_one, user_count, 2)
    return pool_last(slots_two, returned_two, start, lens, dense_out, 5)


def solution(mesh):
    in_specs = (
        P(("row", "col"), None),
        P(("row", "col"), None),
        P(("row", "col"), None),
        P(("row", "col")),
        P(("row", "col"), None),
        P(),
    )
    out_specs = P(("row", "col"), None)
    return jax.shard_map(
        per_device, mesh=mesh, in_specs=in_specs, out_specs=out_specs, check_vma=False
    )
```

time: 160 us -> 122 us (0.76)
  Pallas kernels: 0 us -> 39.7 us
  local copies, waits for them, and re-layouts: 42.1 us -> 3.46 us
  matrix products: 28.6 us -> 0.84 us
  other arithmetic: 15.4 us -> 0.01 us
  starting transfers between devices: 5.63 us -> 11.8 us
  waiting for transfers between devices: 46.2 us -> 43.4 us
    pallas_call x0 -> x5, Pallas kernels: none -> 39.7 us  [the longest x2 28.1 us: fetch(): pl.pallas_call(functools.partial(fetch_kernel, first, count, groups), in_...]
    gather x2 -> x0, local copies, waits for them, and re-layouts: 30.7 us -> none  [per_device(): jnp.take(item_table, arrived.reshape(-1), axis=0)]
    dot_general x5 -> x0, matrix products: 28.4 us -> none  [the longest x1 12.4 us: per_device(): totals = jnp.dot(selector, returned, precision=HIGH)]
    select_n x2 -> x0, other arithmetic: 7.56 us -> none  [per_device(): jnp.take(item_table, arrived.reshape(-1), axis=0)]
    dot_general x1 -> x0, local copies, waits for them, and re-layouts: 6.45 us -> none  [per_device(): jnp.einsum('uho,uhc->uoc', assign, spot, precision=HIGH)]
    all_to_all x1 -> x2, starting transfers between devices: 5.63 us -> 11.8 us  [exchange(): lax.all_to_all(buffer, ('row', 'col'), split_axis=0, concat_axis=0, tiled...]
    and x1 -> x0, local copies, waits for them, and re-layouts: 2.98 us -> none  [per_device(): (rank[:, :, None] == rank_iota) & live_mask[:, :, None]]
    and x3 -> x0, other arithmetic: 2.96 us -> none  [the longest x1 2.51 us: per_device(): (owner_ids[:, :, None] == owner_iota) & live_mask[:, :, None]]
  transfers between devices with their start and end apart: 1 -> 2, of which waited for: 1 -> 2; matrix products, arithmetic and copies ran while one was open for 10% -> 2% of each run, Pallas kernels for 0% -> 17%
where the time goes in v1:
time: 122 us; the launch traced here: 121 us
  waiting for transfers between devices  43.4 us (36%)
  Pallas kernels  39.7 us (33%)
  blocking collectives  21.5 us (18%)
  starting transfers between devices  11.8 us (10%)
  local copies, waits for them, and re-layouts  3.46 us (3%)
    all_to_all x2, waiting for transfers between devices, exchange(): lax.all_to_all(buffer, ('row', 'col'), split_axis=0, concat_axis=0, tiled...  43.4 us
    pallas_call x2, Pallas kernels, fetch(): pl.pallas_call(functools.partial(fetch_kernel, first, count, groups), in_...  28.1 us
    all_to_all x1, blocking collectives, exchange(): lax.all_to_all(buffer, ('row', 'col'), split_axis=0, concat_axis=0, tiled...  21.5 us
    all_to_all x2, starting transfers between devices, exchange(): lax.all_to_all(buffer, ('row', 'col'), split_axis=0, concat_axis=0, tiled...  11.8 us
    pallas_call x1, Pallas kernels, pool_last(): pl.pallas_call(pool_last_kernel, grid=(steps,), in_specs=[pl.BlockSpec((1...  5.03 us
    pallas_call x1, Pallas kernels, route(): pl.pallas_call(route_kernel, in_specs=[pl.BlockSpec(memory_space=pltpu.SM...  4.25 us
  transfers between devices with their start and end apart: 2, of which 2 were waited for; matrix products, arithmetic and copies ran while one was open for 2% of the time, Pallas kernels for 17%

profile of v1, /device:TPU:1, one launch (start us, length us, event | category | flops | bytes accessed | tf_op | source)
XLA Modules:
  0.0 120.9 jit_solution(3071214965713624360)
XLA Ops:
  0.0 0.0 copy-start
  0.0 4.3 %route.1 = (s32[128,128]{1,0:T(8,128)}, s32[128,128]{1,0:T(8,128)}) custom-call(s32[1,1]{1,0:T(1,128)} %bitcast.me_ref, s32[50,128]{1,0:T(8,128)} %bitcast.17, s32[50,128]{1,0:T(8,128)} %bitcast.18, s32[1,128]{1,0:T(1,128)} %bitcast.19), custom_call_target="tpu_custom_call" | custom-call | tf_op jit(solution)/shard_map/route/pallas_call | solution.py:68
  4.3 21.5 %all_to_all.15.wanted_ref = s32[128,1,128]{2,1,0:T(1,128)} all-to-all(s32[128,1,128]{2,1,0:T(1,128)} %bitcast.16), channel_id=1, replica_groups=mesh['row'=8,'col'=16] {'row','col'}, dimensions={0} | all-to-all | bytes 131072 | tf_op jit(solution)/shard_map/all_to_all | solution.py:20
  25.8 9.4 %fetch.3 = f32[2560,128]{1,0:T(8,128)} custom-call(s32[128,1,128]{2,1,0:T(1,128)} %all_to_all.15.wanted_ref, f32[40960,128]{1,0:T(8,128)} %table_ref.3), custom_call_target="tpu_custom_call" | custom-call | flops 10240000 | bytes 2621440 | tf_op jit(solution)/shard_map/fetch/pallas_call | solution.py:124
  35.2 4.3 %all-to-all-start.2 = ((f32[128,20,1,128]{3,2,1,0:T(1,128)}), f32[128,20,1,128]{3,2,1,0:T(1,128)S(1)}, u32[]{:S(2)}, u32[]{:S(2)}) async-start(f32[128,20,1,128]{3,2,1,0:T(1,128)} %bitcast.14), calls=%async_computation.2 | async-start | bytes 2621440 | tf_op jit(solution)/shard_map/all_to_all | solution.py:20
  39.5 18.7 %fetch.2 = f32[7040,128]{1,0:T(8,128)} custom-call(s32[128,1,128]{2,1,0:T(1,128)} %all_to_all.15.wanted_ref, f32[40960,128]{1,0:T(8,128)} %table_ref.3), custom_call_target="tpu_custom_call" | custom-call | flops 28160000 | bytes 7208960 | tf_op jit(solution)/shard_map/fetch/pallas_call | solution.py:124
  58.2 2.9 %all-to-all-done.2 = f32[128,20,1,128]{3,2,1,0:T(1,128)S(1)} async-done(((f32[128,20,1,128]{3,2,1,0:T(1,128)}), f32[128,20,1,128]{3,2,1,0:T(1,128)S(1)}, u32[]{:S(2)}, u32[]{:S(2)}) %all-to-all-start.2) | async-done | bytes 1310752 | tf_op jit(solution)/shard_map/all_to_all | solution.py:20
  61.1 0.0 copy-start.1
  61.1 0.0 copy-start.3
  61.1 0.0 copy-start.2
  61.1 0.0 copy-start.4
  61.1 1.1 copy-done.1
  62.2 7.5 %all-to-all-start.1 = ((f32[128,55,1,128]{3,2,1,0:T(1,128)}), f32[128,55,1,128]{3,2,1,0:T(1,128)}, u32[]{:S(2)}, u32[]{:S(2)}) async-start(f32[128,55,1,128]{3,2,1,0:T(1,128)} %bitcast.12), calls=%async_computation.1 | async-start | bytes 7208960 | tf_op jit(solution)/shard_map/all_to_all | solution.py:20
  69.8 0.0 copy-done.3
  69.8 0.0 copy-done.2
  69.8 0.1 slice.6
  69.9 0.8 reshape.27.slot_ref
  70.7 0.7 reshape.31.slot_ref
  71.4 0.0 copy-done
  71.5 0.0 copy-done.4
  71.5 0.8 divide_multiply_fusion.dense_ref
  72.3 2.3 %pool_first.1.start_ref = f32[128,256]{1,0:T(8,128)} custom-call(s32[1,2560]{1,0:T(1,128)} %reshape.31.slot_ref, f32[2560,128]{1,0:T(8,128)} %bitcast.13), custom_call_target="tpu_custom_call" | custom-call | flops 10240000 | bytes 1310720 | tf_op jit(solution)/shard_map/pool_first/pallas_call | solution.py:181
  74.6 40.6 %all-to-all-done.1 = f32[128,55,1,128]{3,2,1,0:T(1,128)} async-done(((f32[128,55,1,128]{3,2,1,0:T(1,128)}), f32[128,55,1,128]{3,2,1,0:T(1,128)}, u32[]{:S(2)}, u32[]{:S(2)}) %all-to-all-start.1) | async-done | bytes 3604512 | tf_op jit(solution)/shard_map/all_to_all | solution.py:20
  115.2 0.7 broadcast_in_dim.10.len_ref
  115.9 5.0 %pool_last.1 = f32[128,384]{1,0:T(8,128)} custom-call(s32[1,7040]{1,0:T(1,128)} %reshape.27.slot_ref, f32[7040,128]{1,0:T(8,128)} %bitcast.6.rows_ref, f32[128,256]{1,0:T(8,128)} %pool_first.1.start_ref, f32[128,128]{1,0:T(8,128)} %broadcast_in_dim.10.len_ref, f32[128,256]{1,0:T(8,128)} %divide_multiply_fusion.dense_ref), custom_call_target="tpu_custom_call" | custom-call | tf_op jit(solution)/shard_map/pool_last/pallas_call | solution.py:196
  (1 shorter events, 0.0 us)
Async XLA Ops:
  0.0 71.5 %copy-start = (bf16[256,256]{1,0:T(8,128)(2,1)S(1)}, bf16[256,256]{1,0:T(8,128)(2,1)}, u32[]{:S(2)}) copy-start(bf16[256,256]{1,0:T(8,128)(2,1)} %param.11) | copy-start | bytes 393220
  35.2 25.9 %all-to-all-start.2 = ((f32[128,20,1,128]{3,2,1,0:T(1,128)}), f32[128,20,1,128]{3,2,1,0:T(1,128)S(1)}, u32[]{:S(2)}, u32[]{:S(2)}) async-start(f32[128,20,1,128]{3,2,1,0:T(1,128)} %bitcast.14), calls=%async_computation.2 | async-start | bytes 2621440 | tf_op jit(solution)/shard_map/all_to_all | solution.py:20
  61.1 1.1 copy-start.1
  61.1 8.7 %copy-start.3 = (s32[128]{0:T(128)S(1)}, s32[128]{0:T(128)}, u32[]{:S(2)}) copy-start(s32[128]{0:T(128)} %param.9) | copy-start | bytes 1540
  61.1 8.7 %copy-start.2 = (s32[128,128]{1,0:T(8,128)S(1)}, s32[128,128]{1,0:T(8,128)}, u32[]{:S(2)}) copy-start(s32[128,128]{1,0:T(8,128)} %get-tuple-element.7) | copy-start | bytes 196612
  61.1 10.3 %copy-start.4 = (bf16[128,256]{1,0:T(8,128)(2,1)S(1)}, bf16[128,256]{1,0:T(8,128)(2,1)}, u32[]{:S(2)}) copy-start(bf16[128,256]{1,0:T(8,128)(2,1)} %param.10) | copy-start | bytes 196612
  62.2 52.9 %all-to-all-start.1 = ((f32[128,55,1,128]{3,2,1,0:T(1,128)}), f32[128,55,1,128]{3,2,1,0:T(1,128)}, u32[]{:S(2)}, u32[]{:S(2)}) async-start(f32[128,55,1,128]{3,2,1,0:T(1,128)} %bitcast.12), calls=%async_computation.1 | async-start | bytes 7208960 | tf_op jit(solution)/shard_map/all_to_all | solution.py:20

commit v2 on v1

v2 whole, which is shorter than its diff:
```python
import functools

import jax
import jax.numpy as jnp
from jax import lax
from jax.experimental import pallas as pl
from jax.experimental.pallas import tpu as pltpu
from jax.sharding import PartitionSpec as P

SLOT_PAD = 80
LANES = 128
FIRST_SLOTS = 20
PIECE = 1280


def round_up(value, unit):
    return (value + unit - 1) // unit * unit


def exchange(buffer):
    return lax.all_to_all(buffer, ("row", "col"), split_axis=0, concat_axis=0, tiled=True)


def route_kernel(me_ref, owner_ref, row_ref, len_ref, rows_out, users_out, assign_ref, value_ref):
    hist_len, user_count = owner_ref.shape
    owner_count = rows_out.shape[0]
    span = 2 * user_count
    lens = jnp.concatenate([len_ref[...], len_ref[...]], axis=1)
    owner_iota = lax.broadcasted_iota(jnp.int32, (owner_count, span), 0)
    slot_iota = lax.broadcasted_iota(jnp.int32, (SLOT_PAD, span), 0)
    place_iota = lax.broadcasted_iota(jnp.int32, (1, span), 1)
    second = (place_iota >= user_count).astype(jnp.int32)
    name = (place_iota - second * user_count + 1).astype(jnp.float32)
    earlier = lax.broadcasted_iota(jnp.int32, (span, span), 0)
    later = lax.broadcasted_iota(jnp.int32, (span, span), 1)
    counter = jnp.where(earlier < later, 1.0, 0.0).astype(jnp.bfloat16)
    offset = jnp.zeros((owner_count, 1), jnp.float32)
    for h in range(0, hist_len, 2):
        lanes = slice(h * user_count, h * user_count + span)
        pair = jnp.concatenate([owner_ref[h : h + 1, :], owner_ref[h + 1 : h + 2, :]], axis=1)
        owners = jnp.where(h + second < lens, pair, -1)
        hits = owners == owner_iota
        assign = jnp.where(hits, 1.0, 0.0)
        assign_ref[:, lanes] = assign.astype(jnp.bfloat16)
        counts = jnp.dot(assign_ref[:, lanes], counter, preferred_element_type=jnp.float32)
        rank = jnp.sum(jnp.where(hits, counts + offset, 0.0), axis=0, keepdims=True).astype(jnp.int32)
        offset = offset + counts[:, span - 1 :] + assign[:, span - 1 :]
        spot = rank == slot_iota
        rows = jnp.concatenate([row_ref[h : h + 1, :], row_ref[h + 1 : h + 2, :]], axis=1)
        high = (rows >> 8).astype(jnp.float32)
        low = (rows & 255).astype(jnp.float32)
        for part, content in enumerate((high, low, name)):
            value_ref[part * SLOT_PAD : (part + 1) * SLOT_PAD, lanes] = jnp.where(
                spot, content, 0.0
            ).astype(jnp.bfloat16)
    packed = lax.dot_general(
        assign_ref[...], value_ref[...], (((1,), (1,)), ((), ())), preferred_element_type=jnp.float32
    )
    names = packed[:, 2 * SLOT_PAD :]
    spare = me_ref[0, 0] * SLOT_PAD + lax.broadcasted_iota(jnp.int32, names.shape, 1)
    table_rows = (packed[:, :SLOT_PAD] * 256.0 + packed[:, SLOT_PAD : 2 * SLOT_PAD]).astype(jnp.int32)
    table_rows = jnp.where(names > 0.0, table_rows, spare)
    fill = jnp.zeros((owner_count, LANES - SLOT_PAD), jnp.int32)
    rows_out[...] = jnp.concatenate([table_rows, fill], axis=1)
    users_out[...] = jnp.concatenate([names.astype(jnp.int32), fill], axis=1)


def route(me, owner_t, row_t, lengths, owner_count):
    hist_len, user_count = owner_t.shape
    pos_count = hist_len * user_count
    shape = jax.ShapeDtypeStruct((owner_count, LANES), jnp.int32)
    return pl.pallas_call(
        route_kernel,
        in_specs=[
            pl.BlockSpec(memory_space=pltpu.SMEM),
            pl.BlockSpec(memory_space=pltpu.VMEM),
            pl.BlockSpec(memory_space=pltpu.VMEM),
            pl.BlockSpec(memory_space=pltpu.VMEM),
        ],
        out_shape=(shape, shape),
        scratch_shapes=[
            pltpu.VMEM((owner_count, pos_count), jnp.bfloat16),
            pltpu.VMEM((3 * SLOT_PAD, pos_count), jnp.bfloat16),
        ],
        name="route",
    )(jnp.full((1, 1), me, jnp.int32), owner_t, row_t, lengths.reshape(1, user_count))


def fetch_kernel(first, count, groups, wanted_ref, table_ref, out_ref, rows_ref, stage_ref, row_sems, in_sems, out_sems):
    sources = wanted_ref.shape[0]
    per_group = sources // groups
    span = per_group * count

    def learn(group):
        place = pl.ds(group * per_group, per_group)
        return pltpu.make_async_copy(wanted_ref.at[place], rows_ref.at[place], row_sems.at[group])

    def issue(group):
        def one_source(index, carry):
            source = group * per_group + index
            for c in range(count):
                pltpu.make_async_copy(
                    table_ref.at[pl.ds(rows_ref[source, 0, first + c], 1), :],
                    stage_ref.at[pl.ds(source * count + c, 1), :],
                    in_sems.at[group],
                ).start(priority=c % 2)
            return carry

        lax.fori_loop(0, per_group, one_source, 0)

    def store(group):
        place = pl.ds(group * span, span)
        return pltpu.make_async_copy(stage_ref.at[place, :], out_ref.at[place, :], out_sems.at[group])

    def arrive(group):
        place = pl.ds(group * span, span)
        pltpu.make_async_copy(table_ref.at[pl.ds(0, span), :], stage_ref.at[place, :], in_sems.at[group]).wait()
        store(group).start()

    for group in range(groups):
        learn(group).start()
    for group in range(groups):
        learn(group).wait()
        issue(group)
        if group > 0:
            arrive(group - 1)
    arrive(groups - 1)
    for group in range(groups):
        store(group).wait()


def fetch(wanted, item_table, first, count, groups):
    sources = wanted.shape[0]
    dim = item_table.shape[1]
    return pl.pallas_call(
        functools.partial(fetch_kernel, first, count, groups),
        in_specs=[pl.BlockSpec(memory_space=pltpu.HBM), pl.BlockSpec(memory_space=pltpu.HBM)],
        out_specs=pl.BlockSpec(memory_space=pltpu.HBM),
        out_shape=jax.ShapeDtypeStruct((sources * count, dim), jnp.float32),
        scratch_shapes=[
            pltpu.SMEM(wanted.shape, jnp.int32),
            pltpu.VMEM((sources * count, dim), jnp.float32),
            pltpu.SemaphoreType.DMA((groups,)),
            pltpu.SemaphoreType.DMA((groups,)),
            pltpu.SemaphoreType.DMA((groups,)),
        ],
        cost_estimate=pl.CostEstimate(
            flops=sources * count * 4000, bytes_accessed=sources * count * dim * 8, transcendentals=0
        ),
        compiler_params=pltpu.CompilerParams(vmem_limit_bytes=63 * 2**20),
        name="fetch",
    )(wanted, item_table)


def sum_rows(slot_ref, rows_ref, stage_ref, sems, before):
    user_count = before.shape[0]
    count = rows_ref.shape[0]
    starts = list(range(0, count, PIECE))
    copies = []
    for part, start in enumerate(starts):
        place = pl.ds(start, min(PIECE, count - start))
        copies.append(pltpu.make_async_copy(rows_ref.at[place, :], stage_ref.at[place, :], sems.at[part]))
        copies[-1].start()
    total = before
    for start, copy in zip(starts, copies):
        length = min(PIECE, count - start)
        users = lax.broadcasted_iota(jnp.int32, (user_count, length), 0) + 1
        selector = jnp.where(slot_ref[:, start : start + length] == users, 1.0, 0.0).astype(jnp.bfloat16)
        copy.wait()
        rows = stage_ref[start : start + length, :]
        high = rows.astype(jnp.bfloat16)
        low = (rows - high.astype(jnp.float32)).astype(jnp.bfloat16)
        total = total + jnp.dot(
            selector, jnp.concatenate([high, low], axis=1), preferred_element_type=jnp.float32
        )
    return total


def pool_first_kernel(slot_ref, rows_ref, total_ref, stage_ref, sems):
    total_ref[...] = sum_rows(slot_ref, rows_ref, stage_ref, sems, jnp.zeros(total_ref.shape, jnp.float32))


def pool_last_kernel(slot_ref, rows_ref, start_ref, len_ref, dense_ref, out_ref, stage_ref, sems):
    dim = rows_ref.shape[1]
    user_count = out_ref.shape[0]
    total = sum_rows(slot_ref, rows_ref, stage_ref, sems, start_ref[...])
    here = lax.broadcasted_iota(jnp.int32, (user_count, user_count), 0)
    there = lax.broadcasted_iota(jnp.int32, (user_count, user_count), 1)
    spread = jnp.where(here == there, len_ref[...].astype(jnp.float32), 0.0)
    lens = jnp.sum(spread, axis=1, keepdims=True)
    out_ref[:, :dim] = (total[:, :dim] + total[:, dim:]) / lens
    out_ref[:, dim:] = dense_ref[...]


def pool_scratch(count, dim):
    return [pltpu.VMEM((count, dim), jnp.float32), pltpu.SemaphoreType.DMA((pl.cdiv(count, PIECE),))]


def pool_first(slots, rows, user_count):
    count, dim = rows.shape
    return pl.pallas_call(
        pool_first_kernel,
        in_specs=[pl.BlockSpec(memory_space=pltpu.VMEM), pl.BlockSpec(memory_space=pltpu.HBM)],
        out_shape=jax.ShapeDtypeStruct((user_count, 2 * dim), jnp.float32),
        scratch_shapes=pool_scratch(count, dim),
        cost_estimate=pl.CostEstimate(flops=count * 4000, bytes_accessed=count * dim * 4, transcendentals=0),
        name="pool_first",
    )(slots, rows)


def pool_last(slots, rows, start, lengths, dense_out):
    count, dim = rows.shape
    user_count, dense_dim = dense_out.shape
    vmem = pl.BlockSpec(memory_space=pltpu.VMEM)
    return pl.pallas_call(
        pool_last_kernel,
        in_specs=[vmem, pl.BlockSpec(memory_space=pltpu.HBM), vmem, vmem, vmem],
        out_shape=jax.ShapeDtypeStruct((user_count, dim + dense_dim), jnp.float32),
        scratch_shapes=pool_scratch(count, dim),
        name="pool_last",
    )(slots, rows, start, lengths.reshape(1, user_count), dense_out)


def per_device(item_table, owner_ids, row_ids, lengths, dense_input, w_bottom):
    user_count, hist_len = owner_ids.shape
    dim = item_table.shape[1]
    owner_count = lax.axis_size("row") * lax.axis_size("col")
    capacity = 3 * user_count * hist_len // (2 * owner_count)
    ahead = FIRST_SLOTS
    behind = capacity - ahead
    me = lax.axis_index("row") * lax.axis_size("col") + lax.axis_index("col")
    table_rows, slot_users = route(me, owner_ids.T, row_ids.T, lengths, owner_count)
    wanted = exchange(table_rows.reshape(owner_count, 1, LANES))
    fetched_one = fetch(wanted, item_table, 0, ahead, 8)
    fetched_two = fetch(wanted, item_table, ahead, behind, 8)
    returned_one = exchange(fetched_one.reshape(owner_count, ahead, 1, dim)).reshape(-1, dim)
    returned_two = exchange(fetched_two.reshape(owner_count, behind, 1, dim)).reshape(-1, dim)
    slots_one = slot_users[:, :ahead].reshape(1, owner_count * ahead)
    slots_two = slot_users[:, ahead:capacity].reshape(1, owner_count * behind)
    hidden = jnp.dot(dense_input, w_bottom, preferred_element_type=jnp.float32)
    dense_out = jax.nn.silu(hidden)
    start = pool_first(slots_one, returned_one, user_count)
    return pool_last(slots_two, returned_two, start, lengths, dense_out)


def solution(mesh):
    in_specs = (
        P(("row", "col"), None),
        P(("row", "col"), None),
        P(("row", "col"), None),
        P(("row", "col")),
        P(("row", "col"), None),
        P(),
    )
    out_specs = P(("row", "col"), None)
    return jax.shard_map(
        per_device, mesh=mesh, in_specs=in_specs, out_specs=out_specs, check_vma=False
    )
```

time: 122 us -> 118 us (0.967)
  Pallas kernels: 39.7 us -> 37.3 us
  local copies, waits for them, and re-layouts: 3.46 us -> 1.64 us
    pallas_call x2, Pallas kernels: 28.1 us -> 26.4 us  [fetch(): pl.pallas_call(functools.partial(fetch_kernel, first, count, groups), in_...]
  transfers between devices with their start and end apart: 2 -> 2, of which waited for: 2 -> 2; matrix products, arithmetic and copies ran while one was open for 2% -> 2% of each run, Pallas kernels for 17% -> 18%
where the time goes in v2:
time: 118 us; the launch traced here: 117 us
  waiting for transfers between devices  43.3 us (37%)
  Pallas kernels  37.3 us (32%)
  blocking collectives  21.4 us (18%)
  starting transfers between devices  12.6 us (11%)
  local copies, waits for them, and re-layouts  1.64 us (1%)
    all_to_all x2, waiting for transfers between devices, exchange(): lax.all_to_all(buffer, ('row', 'col'), split_axis=0, concat_axis=0, tiled...  43.3 us
    pallas_call x2, Pallas kernels, fetch(): pl.pallas_call(functools.partial(fetch_kernel, first, count, groups), in_...  26.4 us
    all_to_all x1, blocking collectives, exchange(): lax.all_to_all(buffer, ('row', 'col'), split_axis=0, concat_axis=0, tiled...  21.4 us
    all_to_all x2, starting transfers between devices, exchange(): lax.all_to_all(buffer, ('row', 'col'), split_axis=0, concat_axis=0, tiled...  12.6 us
    pallas_call x1, Pallas kernels, pool_last(): pl.pallas_call(pool_last_kernel, in_specs=[vmem, pl.BlockSpec(memory_spac...  4.22 us
    pallas_call x1, Pallas kernels, route(): pl.pallas_call(route_kernel, in_specs=[pl.BlockSpec(memory_space=pltpu.SM...  3.67 us
    pallas_call x1, Pallas kernels, pool_first(): pl.pallas_call(pool_first_kernel, in_specs=[pl.BlockSpec(memory_space=plt...  3 us
  transfers between devices with their start and end apart: 2, of which 2 were waited for; matrix products, arithmetic and copies ran while one was open for 2% of the time, Pallas kernels for 18%

profile of v2, /device:TPU:1, one launch (start us, length us, event | category | flops | bytes accessed | tf_op | source)
XLA Modules:
  0.0 117.1 jit_solution(2313663786191195366)
XLA Ops:
  0.0 0.0 copy-start
  0.0 3.7 %route.1 = (s32[128,128]{1,0:T(8,128)}, s32[128,128]{1,0:T(8,128)}) custom-call(s32[1,1]{1,0:T(1,128)} %bitcast.me_ref, s32[50,128]{1,0:T(8,128)} %bitcast.16, s32[50,128]{1,0:T(8,128)} %bitcast.17, s32[1,128]{1,0:T(1,128)} %bitcast.18), custom_call_target="tpu_custom_call" | custom-call | tf_op jit(solution)/shard_map/route/pallas_call | solution.py:72
  3.7 21.4 %all_to_all.15.wanted_ref = s32[128,1,128]{2,1,0:T(1,128)} all-to-all(s32[128,1,128]{2,1,0:T(1,128)} %bitcast.15), channel_id=1, replica_groups=mesh['row'=8,'col'=16] {'row','col'}, dimensions={0} | all-to-all | bytes 131072 | tf_op jit(solution)/shard_map/all_to_all | solution.py:21
  25.0 8.5 %fetch.3 = f32[2560,128]{1,0:T(8,128)} custom-call(s32[128,1,128]{2,1,0:T(1,128)} %all_to_all.15.wanted_ref, f32[40960,128]{1,0:T(8,128)} %table_ref.3), custom_call_target="tpu_custom_call" | custom-call | flops 10240000 | bytes 2621440 | tf_op jit(solution)/shard_map/fetch/pallas_call | solution.py:135
  33.5 5.5 %all-to-all-start.2 = ((f32[128,20,1,128]{3,2,1,0:T(1,128)}), f32[128,20,1,128]{3,2,1,0:T(1,128)}, u32[]{:S(2)}, u32[]{:S(2)}) async-start(f32[128,20,1,128]{3,2,1,0:T(1,128)} %bitcast.13), calls=%async_computation.2 | async-start | bytes 2621440 | tf_op jit(solution)/shard_map/all_to_all | solution.py:21
  39.0 17.9 %fetch.2 = f32[7040,128]{1,0:T(8,128)} custom-call(s32[128,1,128]{2,1,0:T(1,128)} %all_to_all.15.wanted_ref, f32[40960,128]{1,0:T(8,128)} %table_ref.3), custom_call_target="tpu_custom_call" | custom-call | flops 28160000 | bytes 7208960 | tf_op jit(solution)/shard_map/fetch/pallas_call | solution.py:135
  57.0 3.4 %all-to-all-done.2 = f32[128,20,1,128]{3,2,1,0:T(1,128)} async-done(((f32[128,20,1,128]{3,2,1,0:T(1,128)}), f32[128,20,1,128]{3,2,1,0:T(1,128)}, u32[]{:S(2)}, u32[]{:S(2)}) %all-to-all-start.2) | async-done | bytes 1310752 | tf_op jit(solution)/shard_map/all_to_all | solution.py:21
  60.4 0.0 copy-start.1
  60.4 0.0 copy-start.2
  60.4 7.1 %all-to-all-start.1 = ((f32[128,55,1,128]{3,2,1,0:T(1,128)}), f32[128,55,1,128]{3,2,1,0:T(1,128)}, u32[]{:S(2)}, u32[]{:S(2)}) async-start(f32[128,55,1,128]{3,2,1,0:T(1,128)} %bitcast.12), calls=%async_computation.1 | async-start | bytes 7208960 | tf_op jit(solution)/shard_map/all_to_all | solution.py:21
  67.5 0.0 copy-done.1
  67.5 0.1 slice.6
  67.5 0.8 reshape.26.slot_ref
  68.4 0.7 reshape.30.slot_ref
  69.1 0.0 copy-done
  69.1 0.0 copy-done.2
  69.1 0.8 divide_multiply_fusion.dense_ref
  69.9 3.0 %pool_first.1.start_ref = f32[128,256]{1,0:T(8,128)} custom-call(s32[1,2560]{1,0:T(1,128)} %reshape.30.slot_ref, f32[2560,128]{1,0:T(8,128)} %bitcast.8.rows_ref), custom_call_target="tpu_custom_call" | custom-call | flops 10240000 | bytes 1310720 | tf_op jit(solution)/shard_map/pool_first/pallas_call | solution.py:201
  73.0 39.9 %all-to-all-done.1 = f32[128,55,1,128]{3,2,1,0:T(1,128)} async-done(((f32[128,55,1,128]{3,2,1,0:T(1,128)}), f32[128,55,1,128]{3,2,1,0:T(1,128)}, u32[]{:S(2)}, u32[]{:S(2)}) %all-to-all-start.1) | async-done | bytes 3604512 | tf_op jit(solution)/shard_map/all_to_all | solution.py:21
  112.8 4.2 %pool_last.1 = f32[128,384]{1,0:T(8,128)} custom-call(s32[1,7040]{1,0:T(1,128)} %reshape.26.slot_ref, f32[7040,128]{1,0:T(8,128)} %bitcast.6.rows_ref, f32[128,256]{1,0:T(8,128)} %pool_first.1.start_ref, s32[1,128]{1,0:T(1,128)} %bitcast.19, f32[128,256]{1,0:T(8,128)} %divide_multiply_fusion.dense_ref), custom_call_target="tpu_custom_call" | custom-call | tf_op jit(solution)/shard_map/pool_last/pallas_call | solution.py:215
Async XLA Ops:
  0.0 69.1 %copy-start = (bf16[256,256]{1,0:T(8,128)(2,1)S(1)}, bf16[256,256]{1,0:T(8,128)(2,1)}, u32[]{:S(2)}) copy-start(bf16[256,256]{1,0:T(8,128)(2,1)} %param.11) | copy-start | bytes 393220
  33.5 26.8 %all-to-all-start.2 = ((f32[128,20,1,128]{3,2,1,0:T(1,128)}), f32[128,20,1,128]{3,2,1,0:T(1,128)}, u32[]{:S(2)}, u32[]{:S(2)}) async-start(f32[128,20,1,128]{3,2,1,0:T(1,128)} %bitcast.13), calls=%async_computation.2 | async-start | bytes 2621440 | tf_op jit(solution)/shard_map/all_to_all | solution.py:21
  60.4 7.1 %copy-start.1 = (s32[128,128]{1,0:T(8,128)S(1)}, s32[128,128]{1,0:T(8,128)}, u32[]{:S(2)}) copy-start(s32[128,128]{1,0:T(8,128)} %get-tuple-element.7) | copy-start | bytes 196612
  60.4 8.8 %copy-start.2 = (bf16[128,256]{1,0:T(8,128)(2,1)S(1)}, bf16[128,256]{1,0:T(8,128)(2,1)}, u32[]{:S(2)}) copy-start(bf16[128,256]{1,0:T(8,128)(2,1)} %param.10) | copy-start | bytes 196612
  60.4 52.5 %all-to-all-start.1 = ((f32[128,55,1,128]{3,2,1,0:T(1,128)}), f32[128,55,1,128]{3,2,1,0:T(1,128)}, u32[]{:S(2)}, u32[]{:S(2)}) async-start(f32[128,55,1,128]{3,2,1,0:T(1,128)} %bitcast.12), calls=%async_computation.1 | async-start | bytes 7208960 | tf_op jit(solution)/shard_map/all_to_all | solution.py:21

commit v3 on v2

--- a/solution.py
+++ b/solution.py
@@ -9,8 +9,8 @@
 
 SLOT_PAD = 80
 LANES = 128
-FIRST_SLOTS = 20
 PIECE = 1280
+VMEM_LIMIT = 60 * 2**20
 
 
 def round_up(value, unit):
@@ -82,11 +82,13 @@
             pltpu.VMEM((owner_count, pos_count), jnp.bfloat16),
             pltpu.VMEM((3 * SLOT_PAD, pos_count), jnp.bfloat16),
         ],
+        compiler_params=pltpu.CompilerParams(vmem_limit_bytes=VMEM_LIMIT),
         name="route",
     )(jnp.full((1, 1), me, jnp.int32), owner_t, row_t, lengths.reshape(1, user_count))
 
 
-def fetch_kernel(first, count, groups, wanted_ref, table_ref, out_ref, rows_ref, stage_ref, row_sems, in_sems, out_sems):
+def fetch_kernel(count, groups, wanted_ref, table_ref, out_ref, rows_ref, near_ref, stage_ref, row_sems, table_sems, out_sems):
+    part = table_ref.shape[0] // groups
     sources = wanted_ref.shape[0]
     per_group = sources // groups
     span = per_group * count
@@ -95,61 +97,55 @@
         place = pl.ds(group * per_group, per_group)
         return pltpu.make_async_copy(wanted_ref.at[place], rows_ref.at[place], row_sems.at[group])
 
-    def issue(group):
+    def store(group):
+        place = pl.ds(group * span, span)
+        return pltpu.make_async_copy(stage_ref.at[place], out_ref.at[place], out_sems.at[group])
+
+    def approach(group):
+        place = pl.ds(group * part, part)
+        return pltpu.make_async_copy(table_ref.at[place], near_ref.at[place], table_sems.at[group])
+
+    for group in range(groups):
+        approach(group).start(priority=group % 2)
+    for group in range(groups):
+        learn(group).start()
+    for group in range(groups):
+        learn(group).wait()
+    for group in range(groups):
+        approach(group).wait()
+    for group in range(groups):
+
         def one_source(index, carry):
             source = group * per_group + index
             for c in range(count):
-                pltpu.make_async_copy(
-                    table_ref.at[pl.ds(rows_ref[source, 0, first + c], 1), :],
-                    stage_ref.at[pl.ds(source * count + c, 1), :],
-                    in_sems.at[group],
-                ).start(priority=c % 2)
+                stage_ref[pl.ds(source * count + c, 1)] = near_ref[pl.ds(rows_ref[source, 0, c], 1)]
             return carry
 
         lax.fori_loop(0, per_group, one_source, 0)
-
-    def store(group):
-        place = pl.ds(group * span, span)
-        return pltpu.make_async_copy(stage_ref.at[place, :], out_ref.at[place, :], out_sems.at[group])
-
-    def arrive(group):
-        place = pl.ds(group * span, span)
-        pltpu.make_async_copy(table_ref.at[pl.ds(0, span), :], stage_ref.at[place, :], in_sems.at[group]).wait()
         store(group).start()
-
-    for group in range(groups):
-        learn(group).start()
-    for group in range(groups):
-        learn(group).wait()
-        issue(group)
-        if group > 0:
-            arrive(group - 1)
-    arrive(groups - 1)
     for group in range(groups):
         store(group).wait()
 
 
-def fetch(wanted, item_table, first, count, groups):
+def fetch(wanted, table, count, groups):
     sources = wanted.shape[0]
-    dim = item_table.shape[1]
+    shape = (sources * count,) + table.shape[1:]
     return pl.pallas_call(
-        functools.partial(fetch_kernel, first, count, groups),
-        in_specs=[pl.BlockSpec(memory_space=pltpu.HBM), pl.BlockSpec(memory_space=pltpu.HBM)],
-        out_specs=pl.BlockSpec(memory_space=pltpu.HBM),
-        out_shape=jax.ShapeDtypeStruct((sources * count, dim), jnp.float32),
+        functools.partial(fetch_kernel, count, groups),
+        in_specs=[pl.BlockSpec(memory_space=pl.ANY), pl.BlockSpec(memory_space=pl.ANY)],
+        out_specs=pl.BlockSpec(memory_space=pl.ANY),
+        out_shape=jax.ShapeDtypeStruct(shape, jnp.float32),
         scratch_shapes=[
             pltpu.SMEM(wanted.shape, jnp.int32),
-            pltpu.VMEM((sources * count, dim), jnp.float32),
+            pltpu.VMEM(table.shape, jnp.float32),
+            pltpu.VMEM(shape, jnp.float32),
             pltpu.SemaphoreType.DMA((groups,)),
             pltpu.SemaphoreType.DMA((groups,)),
             pltpu.SemaphoreType.DMA((groups,)),
         ],
-        cost_estimate=pl.CostEstimate(
-            flops=sources * count * 4000, bytes_accessed=sources * count * dim * 8, transcendentals=0
-        ),
-        compiler_params=pltpu.CompilerParams(vmem_limit_bytes=63 * 2**20),
+        compiler_params=pltpu.CompilerParams(vmem_limit_bytes=VMEM_LIMIT),
         name="fetch",
-    )(wanted, item_table)
+    )(wanted, table)
 
 
 def sum_rows(slot_ref, rows_ref, stage_ref, sems, before):
@@ -176,14 +172,10 @@
     return total
 
 
-def pool_first_kernel(slot_ref, rows_ref, total_ref, stage_ref, sems):
-    total_ref[...] = sum_rows(slot_ref, rows_ref, stage_ref, sems, jnp.zeros(total_ref.shape, jnp.float32))
-
-
-def pool_last_kernel(slot_ref, rows_ref, start_ref, len_ref, dense_ref, out_ref, stage_ref, sems):
+def pool_kernel(slot_ref, rows_ref, len_ref, dense_ref, out_ref, stage_ref, sems):
     dim = rows_ref.shape[1]
     user_count = out_ref.shape[0]
-    total = sum_rows(slot_ref, rows_ref, stage_ref, sems, start_ref[...])
+    total = sum_rows(slot_ref, rows_ref, stage_ref, sems, jnp.zeros((user_count, 2 * dim), jnp.float32))
     here = lax.broadcasted_iota(jnp.int32, (user_count, user_count), 0)
     there = lax.broadcasted_iota(jnp.int32, (user_count, user_count), 1)
     spread = jnp.where(here == there, len_ref[...].astype(jnp.float32), 0.0)
@@ -196,29 +188,18 @@
     return [pltpu.VMEM((count, dim), jnp.float32), pltpu.SemaphoreType.DMA((pl.cdiv(count, PIECE),))]
 
 
-def pool_first(slots, rows, user_count):
-    count, dim = rows.shape
-    return pl.pallas_call(
-        pool_first_kernel,
-        in_specs=[pl.BlockSpec(memory_space=pltpu.VMEM), pl.BlockSpec(memory_space=pltpu.HBM)],
-        out_shape=jax.ShapeDtypeStruct((user_count, 2 * dim), jnp.float32),
-        scratch_shapes=pool_scratch(count, dim),
-        cost_estimate=pl.CostEstimate(flops=count * 4000, bytes_accessed=count * dim * 4, transcendentals=0),
-        name="pool_first",
-    )(slots, rows)
-
-
-def pool_last(slots, rows, start, lengths, dense_out):
+def pool(slots, rows, lengths, dense_out):
     count, dim = rows.shape
     user_count, dense_dim = dense_out.shape
     vmem = pl.BlockSpec(memory_space=pltpu.VMEM)
     return pl.pallas_call(
-        pool_last_kernel,
-        in_specs=[vmem, pl.BlockSpec(memory_space=pltpu.HBM), vmem, vmem, vmem],
+        pool_kernel,
+        in_specs=[vmem, pl.BlockSpec(memory_space=pl.ANY), vmem, vmem],
         out_shape=jax.ShapeDtypeStruct((user_count, dim + dense_dim), jnp.float32),
         scratch_shapes=pool_scratch(count, dim),
-        name="pool_last",
-    )(slots, rows, start, lengths.reshape(1, user_count), dense_out)
+        compiler_params=pltpu.CompilerParams(vmem_limit_bytes=VMEM_LIMIT),
+        name="pool",
+    )(slots, rows, lengths.reshape(1, user_count), dense_out)
 
 
 def per_device(item_table, owner_ids, row_ids, lengths, dense_input, w_bottom):
@@ -226,21 +207,16 @@
     dim = item_table.shape[1]
     owner_count = lax.axis_size("row") * lax.axis_size("col")
     capacity = 3 * user_count * hist_len // (2 * owner_count)
-    ahead = FIRST_SLOTS
-    behind = capacity - ahead
+    slot_total = owner_count * capacity
     me = lax.axis_index("row") * lax.axis_size("col") + lax.axis_index("col")
     table_rows, slot_users = route(me, owner_ids.T, row_ids.T, lengths, owner_count)
     wanted = exchange(table_rows.reshape(owner_count, 1, LANES))
-    fetched_one = fetch(wanted, item_table, 0, ahead, 8)
-    fetched_two = fetch(wanted, item_table, ahead, behind, 8)
-    returned_one = exchange(fetched_one.reshape(owner_count, ahead, 1, dim)).reshape(-1, dim)
-    returned_two = exchange(fetched_two.reshape(owner_count, behind, 1, dim)).reshape(-1, dim)
-    slots_one = slot_users[:, :ahead].reshape(1, owner_count * ahead)
-    slots_two = slot_users[:, ahead:capacity].reshape(1, owner_count * behind)
+    fetched = fetch(wanted, item_table.reshape(-1, 1, dim), capacity, 8)
+    returned = exchange(fetched.reshape(owner_count, capacity, 1, dim)).reshape(slot_total, dim)
+    slots = slot_users[:, :capacity].reshape(1, slot_total)
     hidden = jnp.dot(dense_input, w_bottom, preferred_element_type=jnp.float32)
     dense_out = jax.nn.silu(hidden)
-    start = pool_first(slots_one, returned_one, user_count)
-    return pool_last(slots_two, returned_two, start, lengths, dense_out)
+    return pool(slots, returned, lengths, dense_out)
 
 
 def solution(mesh):

time: 118 us -> 112 us (0.949)
  waiting for transfers between devices: 43.3 us -> 57.7 us
  Pallas kernels: 37.3 us -> 24.7 us
  starting transfers between devices: 12.6 us -> 5.51 us
    all_to_all x2 -> x1, waiting for transfers between devices: 43.3 us -> 57.7 us  [exchange(): lax.all_to_all(buffer, ('row', 'col'), split_axis=0, concat_axis=0, tiled...]
    pallas_call x4 -> x2, Pallas kernels: 33.6 us -> 21.1 us  [the longest x1 16.3 us: fetch(): pl.pallas_call(functools.partial(fetch_kernel, count, groups), in_specs=[...]
    all_to_all x2 -> x1, starting transfers between devices: 12.6 us -> 5.51 us  [exchange(): lax.all_to_all(buffer, ('row', 'col'), split_axis=0, concat_axis=0, tiled...]
  transfers between devices with their start and end apart: 2 -> 1, of which waited for: 2 -> 1; matrix products, arithmetic and copies ran while one was open for 2% -> 2% of each run, Pallas kernels for 18% -> 0%
where the time goes in v3:
time: 112 us; the launch traced here: 111 us
  waiting for transfers between devices  57.7 us (52%)
  Pallas kernels  24.7 us (22%)
  blocking collectives  21.5 us (19%)
  starting transfers between devices  5.51 us (5%)
    all_to_all x1, waiting for transfers between devices, exchange(): lax.all_to_all(buffer, ('row', 'col'), split_axis=0, concat_axis=0, tiled...  57.7 us
    all_to_all x1, blocking collectives, exchange(): lax.all_to_all(buffer, ('row', 'col'), split_axis=0, concat_axis=0, tiled...  21.5 us
    pallas_call x1, Pallas kernels, fetch(): pl.pallas_call(functools.partial(fetch_kernel, count, groups), in_specs=[...  16.3 us
    all_to_all x1, starting transfers between devices, exchange(): lax.all_to_all(buffer, ('row', 'col'), split_axis=0, concat_axis=0, tiled...  5.51 us
    pallas_call x1, Pallas kernels, pool(): pl.pallas_call(pool_kernel, in_specs=[vmem, pl.BlockSpec(memory_space=pl....  4.75 us
    pallas_call x1, Pallas kernels, route(): pl.pallas_call(route_kernel, in_specs=[pl.BlockSpec(memory_space=pltpu.SM...  3.67 us
  transfers between devices with their start and end apart: 1, of which 1 were waited for; matrix products, arithmetic and copies ran while one was open for 2% of the time, Pallas kernels for 0%

profile of v3, /device:TPU:1, one launch (start us, length us, event | category | flops | bytes accessed | tf_op | source)
XLA Modules:
  0.0 111.2 jit_solution(11538121392815008968)
XLA Ops:
  0.0 0.0 copy-start
  0.0 3.7 %route.1 = (s32[128,128]{1,0:T(8,128)}, s32[128,128]{1,0:T(8,128)}) custom-call(s32[1,1]{1,0:T(1,128)} %bitcast.me_ref, s32[50,128]{1,0:T(8,128)} %bitcast.15, s32[50,128]{1,0:T(8,128)} %bitcast.16, s32[1,128]{1,0:T(1,128)} %bitcast.17), custom_call_target="tpu_custom_call" | custom-call | tf_op jit(solution)/shard_map/route/pallas_call | solution.py:72
  3.7 21.5 %all_to_all.10.wanted_ref = s32[128,1,128]{2,1,0:T(1,128)} all-to-all(s32[128,1,128]{2,1,0:T(1,128)} %bitcast.14), channel_id=1, replica_groups=mesh['row'=8,'col'=16] {'row','col'}, dimensions={0} | all-to-all | bytes 131072 | tf_op jit(solution)/shard_map/all_to_all | solution.py:21
  25.2 16.3 %fetch.1 = f32[9600,1,128]{2,1,0:T(1,128)} custom-call(s32[128,1,128]{2,1,0:T(1,128)} %all_to_all.10.wanted_ref, f32[40960,1,128]{2,1,0:T(1,128)} %bitcast.11), custom_call_target="tpu_custom_call" | custom-call | tf_op jit(solution)/shard_map/fetch/pallas_call | solution.py:133
  41.5 0.0 copy-start.1
  41.5 0.0 copy-start.2
  41.5 5.5 %all-to-all-start.1 = ((f32[128,75,1,128]{3,2,1,0:T(1,128)}), f32[128,75,1,128]{3,2,1,0:T(1,128)}, u32[]{:S(2)}, u32[]{:S(2)}) async-start(f32[128,75,1,128]{3,2,1,0:T(1,128)} %bitcast.12), calls=%async_computation.1 | async-start | bytes 9830400 | tf_op jit(solution)/shard_map/all_to_all | solution.py:21
  47.0 0.0 copy-done.1
  47.1 0.8 reshape.20.slot_ref
  47.9 0.0 copy-done
  47.9 0.0 copy-done.2
  47.9 0.8 divide_multiply_fusion.dense_ref
  48.7 57.7 %all-to-all-done.1 = f32[128,75,1,128]{3,2,1,0:T(1,128)} async-done(((f32[128,75,1,128]{3,2,1,0:T(1,128)}), f32[128,75,1,128]{3,2,1,0:T(1,128)}, u32[]{:S(2)}, u32[]{:S(2)}) %all-to-all-start.1) | async-done | bytes 4915232 | tf_op jit(solution)/shard_map/all_to_all | solution.py:21
  106.5 4.8 %pool.1 = f32[128,384]{1,0:T(8,128)} custom-call(s32[1,9600]{1,0:T(1,128)} %reshape.20.slot_ref, f32[9600,128]{1,0:T(8,128)} %bitcast.7.rows_ref, s32[1,128]{1,0:T(1,128)} %bitcast.18, f32[128,256]{1,0:T(8,128)} %divide_multiply_fusion.dense_ref), custom_call_target="tpu_custom_call" | custom-call | tf_op jit(solution)/shard_map/pool/pallas_call | solution.py:195
Async XLA Ops:
  0.0 47.9 %copy-start = (bf16[256,256]{1,0:T(8,128)(2,1)S(1)}, bf16[256,256]{1,0:T(8,128)(2,1)}, u32[]{:S(2)}) copy-start(bf16[256,256]{1,0:T(8,128)(2,1)} %param.11) | copy-start | bytes 393220
  41.5 5.5 %copy-start.1 = (s32[128,128]{1,0:T(8,128)S(1)}, s32[128,128]{1,0:T(8,128)}, u32[]{:S(2)}) copy-start(s32[128,128]{1,0:T(8,128)} %get-tuple-element.7) | copy-start | bytes 196612
  41.5 6.4 %copy-start.2 = (bf16[128,256]{1,0:T(8,128)(2,1)S(1)}, bf16[128,256]{1,0:T(8,128)(2,1)}, u32[]{:S(2)}) copy-start(bf16[128,256]{1,0:T(8,128)(2,1)} %param.10) | copy-start | bytes 196612
  41.5 65.0 %all-to-all-start.1 = ((f32[128,75,1,128]{3,2,1,0:T(1,128)}), f32[128,75,1,128]{3,2,1,0:T(1,128)}, u32[]{:S(2)}, u32[]{:S(2)}) async-start(f32[128,75,1,128]{3,2,1,0:T(1,128)} %bitcast.12), calls=%async_computation.1 | async-start | bytes 9830400 | tf_op jit(solution)/shard_map/all_to_all | solution.py:21

commit v4 on v3

--- a/solution.py
+++ b/solution.py
@@ -10,6 +10,7 @@
 SLOT_PAD = 80
 LANES = 128
 PIECE = 1280
+TABLE_PIECES = 8
 VMEM_LIMIT = 60 * 2**20
 
 
@@ -88,7 +89,7 @@
 
 
 def fetch_kernel(count, groups, wanted_ref, table_ref, out_ref, rows_ref, near_ref, stage_ref, row_sems, table_sems, out_sems):
-    part = table_ref.shape[0] // groups
+    part = table_ref.shape[0] // TABLE_PIECES
     sources = wanted_ref.shape[0]
     per_group = sources // groups
     span = per_group * count
@@ -105,23 +106,19 @@
         place = pl.ds(group * part, part)
         return pltpu.make_async_copy(table_ref.at[place], near_ref.at[place], table_sems.at[group])
 
-    for group in range(groups):
+    for group in range(TABLE_PIECES):
         approach(group).start(priority=group % 2)
     for group in range(groups):
         learn(group).start()
     for group in range(groups):
         learn(group).wait()
-    for group in range(groups):
+    for group in range(TABLE_PIECES):
         approach(group).wait()
     for group in range(groups):
 
-        def one_source(index, carry):
-            source = group * per_group + index
+        for source in range(group * per_group, (group + 1) * per_group):
             for c in range(count):
-                stage_ref[pl.ds(source * count + c, 1)] = near_ref[pl.ds(rows_ref[source, 0, c], 1)]
-            return carry
-
-        lax.fori_loop(0, per_group, one_source, 0)
+                stage_ref[source * count + c] = near_ref[rows_ref[source, 0, c]]
         store(group).start()
     for group in range(groups):
         store(group).wait()
@@ -140,7 +137,7 @@
             pltpu.VMEM(table.shape, jnp.float32),
             pltpu.VMEM(shape, jnp.float32),
             pltpu.SemaphoreType.DMA((groups,)),
-            pltpu.SemaphoreType.DMA((groups,)),
+            pltpu.SemaphoreType.DMA((TABLE_PIECES,)),
             pltpu.SemaphoreType.DMA((groups,)),
         ],
         compiler_params=pltpu.CompilerParams(vmem_limit_bytes=VMEM_LIMIT),

time: 112 us -> 108 us (0.964)
  Pallas kernels: 24.7 us -> 21.6 us
    pallas_call x1, Pallas kernels: 16.3 us -> 13.2 us  [fetch(): pl.pallas_call(functools.partial(fetch_kernel, count, groups), in_specs=[...]
where the time goes in v4:
time: 108 us
  waiting for transfers between devices  57.7 us (53%)
  Pallas kernels  21.6 us (20%)
  blocking collectives  21.5 us (20%)
  starting transfers between devices  5.51 us (5%)
    all_to_all x1, waiting for transfers between devices, exchange(): lax.all_to_all(buffer, ('row', 'col'), split_axis=0, concat_axis=0, tiled...  57.7 us
    all_to_all x1, blocking collectives, exchange(): lax.all_to_all(buffer, ('row', 'col'), split_axis=0, concat_axis=0, tiled...  21.5 us
    pallas_call x1, Pallas kernels, fetch(): pl.pallas_call(functools.partial(fetch_kernel, count, groups), in_specs=[...  13.2 us
    all_to_all x1, starting transfers between devices, exchange(): lax.all_to_all(buffer, ('row', 'col'), split_axis=0, concat_axis=0, tiled...  5.51 us
    pallas_call x1, Pallas kernels, pool(): pl.pallas_call(pool_kernel, in_specs=[vmem, pl.BlockSpec(memory_space=pl....  4.75 us
    pallas_call x1, Pallas kernels, route(): pl.pallas_call(route_kernel, in_specs=[pl.BlockSpec(memory_space=pltpu.SM...  3.67 us
  transfers between devices with their start and end apart: 1, of which 1 were waited for; matrix products, arithmetic and copies ran while one was open for 2% of the time, Pallas kernels for 0%

profile of v4, /device:TPU:1, one launch (start us, length us, event | category | flops | bytes accessed | tf_op | source)
XLA Modules:
  0.0 108.1 jit_solution(16024125550582216213)
XLA Ops:
  0.0 0.0 copy-start
  0.0 3.7 %route.1 = (s32[128,128]{1,0:T(8,128)}, s32[128,128]{1,0:T(8,128)}) custom-call(s32[1,1]{1,0:T(1,128)} %bitcast.me_ref, s32[50,128]{1,0:T(8,128)} %bitcast.15, s32[50,128]{1,0:T(8,128)} %bitcast.16, s32[1,128]{1,0:T(1,128)} %bitcast.17), custom_call_target="tpu_custom_call" | custom-call | tf_op jit(solution)/shard_map/route/pallas_call | solution.py:73
  3.7 21.5 %all_to_all.10.wanted_ref = s32[128,1,128]{2,1,0:T(1,128)} all-to-all(s32[128,1,128]{2,1,0:T(1,128)} %bitcast.14), channel_id=1, replica_groups=mesh['row'=8,'col'=16] {'row','col'}, dimensions={0} | all-to-all | bytes 131072 | tf_op jit(solution)/shard_map/all_to_all | solution.py:22
  25.2 13.2 %fetch.1 = f32[9600,1,128]{2,1,0:T(1,128)} custom-call(s32[128,1,128]{2,1,0:T(1,128)} %all_to_all.10.wanted_ref, f32[40960,1,128]{2,1,0:T(1,128)} %bitcast.11), custom_call_target="tpu_custom_call" | custom-call | tf_op jit(solution)/shard_map/fetch/pallas_call | solution.py:130
  38.4 0.0 copy-start.1
  38.4 0.0 copy-start.2
  38.4 5.5 %all-to-all-start.1 = ((f32[128,75,1,128]{3,2,1,0:T(1,128)}), f32[128,75,1,128]{3,2,1,0:T(1,128)}, u32[]{:S(2)}, u32[]{:S(2)}) async-start(f32[128,75,1,128]{3,2,1,0:T(1,128)} %bitcast.12), calls=%async_computation.1 | async-start | bytes 9830400 | tf_op jit(solution)/shard_map/all_to_all | solution.py:22
  44.0 0.0 copy-done.1
  44.0 0.8 reshape.20.slot_ref
  44.8 0.0 copy-done
  44.8 0.0 copy-done.2
  44.8 0.8 divide_multiply_fusion.dense_ref
  45.6 57.7 %all-to-all-done.1 = f32[128,75,1,128]{3,2,1,0:T(1,128)} async-done(((f32[128,75,1,128]{3,2,1,0:T(1,128)}), f32[128,75,1,128]{3,2,1,0:T(1,128)}, u32[]{:S(2)}, u32[]{:S(2)}) %all-to-all-start.1) | async-done | bytes 4915232 | tf_op jit(solution)/shard_map/all_to_all | solution.py:22
  103.4 4.8 %pool.1 = f32[128,384]{1,0:T(8,128)} custom-call(s32[1,9600]{1,0:T(1,128)} %reshape.20.slot_ref, f32[9600,128]{1,0:T(8,128)} %bitcast.7.rows_ref, s32[1,128]{1,0:T(1,128)} %bitcast.18, f32[128,256]{1,0:T(8,128)} %divide_multiply_fusion.dense_ref), custom_call_target="tpu_custom_call" | custom-call | tf_op jit(solution)/shard_map/pool/pallas_call | solution.py:192
Async XLA Ops:
  0.0 44.8 %copy-start = (bf16[256,256]{1,0:T(8,128)(2,1)S(1)}, bf16[256,256]{1,0:T(8,128)(2,1)}, u32[]{:S(2)}) copy-start(bf16[256,256]{1,0:T(8,128)(2,1)} %param.11) | copy-start | bytes 393220
  38.4 5.5 %copy-start.1 = (s32[128,128]{1,0:T(8,128)S(1)}, s32[128,128]{1,0:T(8,128)}, u32[]{:S(2)}) copy-start(s32[128,128]{1,0:T(8,128)} %get-tuple-element.7) | copy-start | bytes 196612
  38.4 6.4 %copy-start.2 = (bf16[128,256]{1,0:T(8,128)(2,1)S(1)}, bf16[128,256]{1,0:T(8,128)(2,1)}, u32[]{:S(2)}) copy-start(bf16[128,256]{1,0:T(8,128)(2,1)} %param.10) | copy-start | bytes 196612
  38.4 65.0 %all-to-all-start.1 = ((f32[128,75,1,128]{3,2,1,0:T(1,128)}), f32[128,75,1,128]{3,2,1,0:T(1,128)}, u32[]{:S(2)}, u32[]{:S(2)}) async-start(f32[128,75,1,128]{3,2,1,0:T(1,128)} %bitcast.12), calls=%async_computation.1 | async-start | bytes 9830400 | tf_op jit(solution)/shard_map/all_to_all | solution.py:22

commit v5 on v4

--- a/solution.py
+++ b/solution.py
@@ -119,7 +119,9 @@
         for source in range(group * per_group, (group + 1) * per_group):
             for c in range(count):
                 stage_ref[source * count + c] = near_ref[rows_ref[source, 0, c]]
-        store(group).start()
+        if group > 0:
+            store(group - 1).start()
+    store(groups - 1).start()
     for group in range(groups):
         store(group).wait()
 
@@ -208,7 +210,7 @@
     me = lax.axis_index("row") * lax.axis_size("col") + lax.axis_index("col")
     table_rows, slot_users = route(me, owner_ids.T, row_ids.T, lengths, owner_count)
     wanted = exchange(table_rows.reshape(owner_count, 1, LANES))
-    fetched = fetch(wanted, item_table.reshape(-1, 1, dim), capacity, 8)
+    fetched = fetch(wanted, item_table.reshape(-1, 1, dim), capacity, 16)
     returned = exchange(fetched.reshape(owner_count, capacity, 1, dim)).reshape(slot_total, dim)
     slots = slot_users[:, :capacity].reshape(1, slot_total)
     hidden = jnp.dot(dense_input, w_bottom, preferred_element_type=jnp.float32)

time: 108 us -> 109 us (level)
  no operation moved by 1% of the time
where the time goes in v5:
time: 109 us; the launch traced here: 108 us
  waiting for transfers between devices  57.7 us (53%)
  Pallas kernels  21.8 us (20%)
  blocking collectives  21.5 us (20%)
  starting transfers between devices  5.51 us (5%)
    all_to_all x1, waiting for transfers between devices, exchange(): lax.all_to_all(buffer, ('row', 'col'), split_axis=0, concat_axis=0, tiled...  57.7 us
    all_to_all x1, blocking collectives, exchange(): lax.all_to_all(buffer, ('row', 'col'), split_axis=0, concat_axis=0, tiled...  21.5 us
    pallas_call x1, Pallas kernels, fetch(): pl.pallas_call(functools.partial(fetch_kernel, count, groups), in_specs=[...  13.4 us
    all_to_all x1, starting transfers between devices, exchange(): lax.all_to_all(buffer, ('row', 'col'), split_axis=0, concat_axis=0, tiled...  5.51 us
    pallas_call x1, Pallas kernels, pool(): pl.pallas_call(pool_kernel, in_specs=[vmem, pl.BlockSpec(memory_space=pl....  4.75 us
    pallas_call x1, Pallas kernels, route(): pl.pallas_call(route_kernel, in_specs=[pl.BlockSpec(memory_space=pltpu.SM...  3.67 us
  transfers between devices with their start and end apart: 1, of which 1 were waited for; matrix products, arithmetic and copies ran while one was open for 2% of the time, Pallas kernels for 0%

profile of v5, /device:TPU:1, one launch (start us, length us, event | category | flops | bytes accessed | tf_op | source)
XLA Modules:
  0.0 108.3 jit_solution(10367454727992091)
XLA Ops:
  0.0 0.0 copy-start
  0.0 3.7 %route.1 = (s32[128,128]{1,0:T(8,128)}, s32[128,128]{1,0:T(8,128)}) custom-call(s32[1,1]{1,0:T(1,128)} %bitcast.me_ref, s32[50,128]{1,0:T(8,128)} %bitcast.15, s32[50,128]{1,0:T(8,128)} %bitcast.16, s32[1,128]{1,0:T(1,128)} %bitcast.17), custom_call_target="tpu_custom_call" | custom-call | tf_op jit(solution)/shard_map/route/pallas_call | solution.py:73
  3.7 21.5 %all_to_all.10.wanted_ref = s32[128,1,128]{2,1,0:T(1,128)} all-to-all(s32[128,1,128]{2,1,0:T(1,128)} %bitcast.14), channel_id=1, replica_groups=mesh['row'=8,'col'=16] {'row','col'}, dimensions={0} | all-to-all | bytes 131072 | tf_op jit(solution)/shard_map/all_to_all | solution.py:22
  25.2 13.4 %fetch.1 = f32[9600,1,128]{2,1,0:T(1,128)} custom-call(s32[128,1,128]{2,1,0:T(1,128)} %all_to_all.10.wanted_ref, f32[40960,1,128]{2,1,0:T(1,128)} %bitcast.11), custom_call_target="tpu_custom_call" | custom-call | tf_op jit(solution)/shard_map/fetch/pallas_call | solution.py:132
  38.6 0.0 copy-start.1
  38.6 0.0 copy-start.2
  38.6 5.5 %all-to-all-start.1 = ((f32[128,75,1,128]{3,2,1,0:T(1,128)}), f32[128,75,1,128]{3,2,1,0:T(1,128)}, u32[]{:S(2)}, u32[]{:S(2)}) async-start(f32[128,75,1,128]{3,2,1,0:T(1,128)} %bitcast.12), calls=%async_computation.1 | async-start | bytes 9830400 | tf_op jit(solution)/shard_map/all_to_all | solution.py:22
  44.1 0.0 copy-done.1
  44.1 0.8 reshape.20.slot_ref
  45.0 0.0 copy-done
  45.0 0.0 copy-done.2
  45.0 0.8 divide_multiply_fusion.dense_ref
  45.8 57.7 %all-to-all-done.1 = f32[128,75,1,128]{3,2,1,0:T(1,128)} async-done(((f32[128,75,1,128]{3,2,1,0:T(1,128)}), f32[128,75,1,128]{3,2,1,0:T(1,128)}, u32[]{:S(2)}, u32[]{:S(2)}) %all-to-all-start.1) | async-done | bytes 4915232 | tf_op jit(solution)/shard_map/all_to_all | solution.py:22
  103.5 4.8 %pool.1 = f32[128,384]{1,0:T(8,128)} custom-call(s32[1,9600]{1,0:T(1,128)} %reshape.20.slot_ref, f32[9600,128]{1,0:T(8,128)} %bitcast.7.rows_ref, s32[1,128]{1,0:T(1,128)} %bitcast.18, f32[128,256]{1,0:T(8,128)} %divide_multiply_fusion.dense_ref), custom_call_target="tpu_custom_call" | custom-call | tf_op jit(solution)/shard_map/pool/pallas_call | solution.py:194
Async XLA Ops:
  0.0 45.0 %copy-start = (bf16[256,256]{1,0:T(8,128)(2,1)S(1)}, bf16[256,256]{1,0:T(8,128)(2,1)}, u32[]{:S(2)}) copy-start(bf16[256,256]{1,0:T(8,128)(2,1)} %param.11) | copy-start | bytes 393220
  38.6 5.5 %copy-start.1 = (s32[128,128]{1,0:T(8,128)S(1)}, s32[128,128]{1,0:T(8,128)}, u32[]{:S(2)}) copy-start(s32[128,128]{1,0:T(8,128)} %get-tuple-element.7) | copy-start | bytes 196612
  38.6 6.4 %copy-start.2 = (bf16[128,256]{1,0:T(8,128)(2,1)S(1)}, bf16[128,256]{1,0:T(8,128)(2,1)}, u32[]{:S(2)}) copy-start(bf16[128,256]{1,0:T(8,128)(2,1)} %param.10) | copy-start | bytes 196612
  38.6 65.0 %all-to-all-start.1 = ((f32[128,75,1,128]{3,2,1,0:T(1,128)}), f32[128,75,1,128]{3,2,1,0:T(1,128)}, u32[]{:S(2)}, u32[]{:S(2)}) async-start(f32[128,75,1,128]{3,2,1,0:T(1,128)} %bitcast.12), calls=%async_computation.1 | async-start | bytes 9830400 | tf_op jit(solution)/shard_map/all_to_all | solution.py:22
